TPU v7x, 32 devices: a whole 2x2x4 slice. The times are simulated.
32 devices in a mesh: dp: 4 (over x, core), rollout: 8 (over z, y).
Axes of the slice: x: 2, y: 2, z: 4, core: 2. Of those that a mesh axis runs over, the one named last changes fastest.
Arguments:
- queries: bfloat16 [32, 512, 2560], P(('dp', 'rollout')), may hold values from -100 to 100
- resp_keys: bfloat16 [32, 512, 512], P(('dp', 'rollout')), may hold values from -5 to 5
- resp_values: bfloat16 [32, 512, 512], P(('dp', 'rollout')), may hold values from -6 to 6
- prompt_keys: bfloat16 [4, 128, 512], P('dp', 'rollout'), may hold values from -6 to 6
- prompt_values: bfloat16 [4, 128, 512], P('dp', 'rollout'), may hold values from -6 to 6
- d_out: bfloat16 [32, 512, 2560], P(('dp', 'rollout')), may hold values from -6 to 6
- lengths: int32 [32], replicated, may hold values from 64 to 512
- owner: int32 [32], replicated, may hold values from 0 to 3
Outputs:
- attn_out: bfloat16 [32, 512, 2560], P(('dp', 'rollout'))
- d_queries: bfloat16 [32, 512, 2560], P(('dp', 'rollout'))
- d_resp_keys: bfloat16 [32, 512, 512], P(('dp', 'rollout'))
- d_resp_values: bfloat16 [32, 512, 512], P(('dp', 'rollout'))
- d_prompt_keys: float32 [4, 128, 512], P('dp', 'rollout')
- d_prompt_values: float32 [4, 128, 512], P('dp', 'rollout')
Inputs may be any that keep to these rules, and one draw needn't show every extreme that they name: `lengths`: rows of a block at or past its length are padding.
All inputs are finite; a program needn't handle non-finite values.
Results may differ from a plain program's by a relative error of at most 0.0071.
Values may be sent and summed in bfloat16 or wider, within the bound.
A program may use at most 128 MiB of HBM per device.

v0:
```python
import functools
import math

import jax
import jax.numpy as jnp
from jax import lax
from jax.experimental import pallas as pl
from jax.experimental.pallas import tpu as pltpu
from jax.sharding import PartitionSpec as P

HEAD_DIM = 128
MESH = pl.DeviceIdType.MESH
ROWS = 256
VMEM = pltpu.VMEM


def greet(groups, shards):
    dp, ro = lax.axis_index("dp"), lax.axis_index("rollout")
    barrier = pltpu.get_barrier_semaphore()
    for k in range(1, groups):
        pl.semaphore_signal(
            barrier, inc=1, device_id={"dp": lax.rem(dp + k, groups)}, device_id_type=MESH
        )
    for k in range(1, shards):
        pl.semaphore_signal(
            barrier, inc=1, device_id={"rollout": lax.rem(ro + k, shards)}, device_id_type=MESH
        )
    pl.semaphore_wait(barrier, groups + shards - 2)


def gather_kernel(groups, shards, owner, pk, pv, out, mine, held, stage, s1, r1, s2, r2):
    dp, ro = lax.axis_index("dp"), lax.axis_index("rollout")
    n = mine.shape[1]
    mine[0] = pk[0]
    mine[1] = pv[0]
    greet(groups, shards)
    first = []
    for k in range(1, groups):
        copy = pltpu.make_async_remote_copy(
            src_ref=mine, dst_ref=held.at[k], send_sem=s1.at[k], recv_sem=r1.at[k],
            device_id={"dp": lax.rem(dp + k, groups)}, device_id_type=MESH,
        )
        copy.start()
        first.append(copy)
    held[0] = mine[...]
    for copy in first:
        copy.wait()

    def rows_of(peer):
        return held[lax.rem(dp - owner[dp * shards + peer] + groups, groups)]

    row = pl.ds(pl.multiple_of(ro * n, n), n)
    second = []
    for k in range(1, shards):
        peer = lax.rem(ro + k, shards)
        stage[k] = rows_of(peer)
        copy = pltpu.make_async_remote_copy(
            src_ref=stage.at[k], dst_ref=out.at[:, row, :], send_sem=s2.at[k], recv_sem=r2.at[k],
            device_id={"rollout": peer}, device_id_type=MESH,
        )
        copy.start()
        second.append(copy)
    out[:, row, :] = rows_of(ro)
    for copy in second:
        copy.wait()


def reduce_kernel(groups, shards, owner, term, dpk, dpv, got, acc, stage, got2, s1, r1, s2, r2):
    dp, ro = lax.axis_index("dp"), lax.axis_index("rollout")
    n = got.shape[2]
    greet(groups, shards)
    first = []
    for k in range(1, shards):
        peer = lax.rem(ro + k, shards)
        copy = pltpu.make_async_remote_copy(
            src_ref=term.at[:, pl.ds(pl.multiple_of(peer * n, n), n), :], dst_ref=got.at[k],
            send_sem=s1.at[k], recv_sem=r1.at[k],
            device_id={"rollout": peer}, device_id_type=MESH,
        )
        copy.start()
        first.append(copy)
    got[0] = term[:, pl.ds(pl.multiple_of(ro * n, n), n), :]
    for copy in first:
        copy.wait()
    for k in range(groups):
        target = lax.rem(dp + k, groups)
        total = jnp.zeros(acc.shape, jnp.float32)
        for j in range(shards):
            source = lax.rem(ro - j + shards, shards)
            pick = (owner[dp * shards + source] == target).astype(jnp.float32)
            total = total + pick * got[j].astype(jnp.float32)
        if k == 0:
            acc[...] = total
        else:
            stage[k] = total.astype(jnp.bfloat16)
    second = []
    for k in range(1, groups):
        copy = pltpu.make_async_remote_copy(
            src_ref=stage.at[k], dst_ref=got2.at[k], send_sem=s2.at[k], recv_sem=r2.at[k],
            device_id={"dp": lax.rem(dp + k, groups)}, device_id_type=MESH,
        )
        copy.start()
        second.append(copy)
    for copy in second:
        copy.wait()
    total = acc[...]
    for k in range(1, groups):
        total = total + got2[k].astype(jnp.float32)
    dpk[0] = total[0]
    dpv[0] = total[1]


def dot(a, b, dims=((1,), (0,))):
    return lax.dot_general(a, b, (dims, ((), ())), preferred_element_type=jnp.float32)


def attend_kernel(group, length, q, d, rk, rv, prompt, out, dq, dk, dv, term,
                  kc, vc, kt, vt, dks, dvs):
    block = q.shape[1]
    pn = prompt.shape[1]
    scale = HEAD_DIM ** -0.5
    live_n = length[0]
    kc[:pn] = prompt[0]
    kc[pn:] = rk[0]
    vc[:pn] = prompt[1]
    vc[pn:] = rv[0]
    kt[...] = kc[...].T
    vt[...] = vc[...].T
    dks[...] = jnp.zeros_like(dks)
    dvs[...] = jnp.zeros_like(dvs)
    lead = lax.broadcasted_iota(jnp.int32, (ROWS, ROWS), 0) <= lax.broadcasted_iota(
        jnp.int32, (ROWS, ROWS), 1
    )

    def head(h):
        cols = pl.ds(pl.multiple_of(h * HEAD_DIM, HEAD_DIM), HEAD_DIM)
        for t in range(block // ROWS):
            rows = pl.ds(t * ROWS, ROWS)
            old, span = pn + t * ROWS, pn + (t + 1) * ROWS
            live = (
                lax.broadcasted_iota(jnp.int32, (ROWS, HEAD_DIM), 0) + t * ROWS < live_n
            )
            qt = q[0, rows, cols]
            g = jnp.where(live, d[0, rows, cols].astype(jnp.float32), 0.0).astype(jnp.bfloat16)
            c = scale * math.log2(math.e)
            sa = dot(kc[:old], qt, ((1,), (1,))) * c
            sb = jnp.where(lead, dot(kc[old:span], qt, ((1,), (1,))) * c, -1e30)
            top = jnp.maximum(
                jnp.max(sa, axis=0, keepdims=True), jnp.max(sb, axis=0, keepdims=True)
            )
            ea, eb = jnp.exp2(sa - top), jnp.exp2(sb - top)
            inv = 1.0 / (
                jnp.sum(ea, axis=0, keepdims=True) + jnp.sum(eb, axis=0, keepdims=True)
            )
            p = jnp.concatenate([ea, eb], axis=0) * inv
            w = p.astype(jnp.bfloat16)
            o = dot(vt[:, :span], w)
            out[0, rows, cols] = jnp.where(live, o.T, 0.0).astype(jnp.bfloat16)
            dp = dot(vc[:span], g, ((1,), (1,)))
            delta = jnp.sum(p * dp, axis=0, keepdims=True)
            ds = (p * (dp - delta)).astype(jnp.bfloat16)
            dq[0, rows, cols] = (dot(kt[:, :span], ds) * scale).T.astype(jnp.bfloat16)
            dks[:span] += dot(ds, qt)
            dvs[:span] += dot(w, g)

    for h in range(group):
        head(h)
    dkf = dks[...] * scale
    dk[0] = dkf[pn:].astype(jnp.bfloat16)
    dv[0] = dvs[pn:].astype(jnp.bfloat16)
    term[0] = dkf[:pn].astype(jnp.bfloat16)
    term[1] = dvs[:pn].astype(jnp.bfloat16)


def per_device(queries, resp_keys, resp_values, prompt_keys, prompt_values, d_out, lengths, owner):
    shards = lax.axis_size("rollout")
    groups = lax.axis_size("dp")
    here = lax.axis_index("dp") * shards + lax.axis_index("rollout")
    n, kw = prompt_keys.shape[1:]
    pn = n * shards
    block, qw = queries.shape[1:]
    heads = kw // HEAD_DIM
    group = qw // kw
    span = pn + block
    smem = pl.BlockSpec(memory_space=pltpu.SMEM)
    vmem = pl.BlockSpec(memory_space=pltpu.VMEM)
    dma = pltpu.SemaphoreType.DMA
    bf16, f32 = jnp.bfloat16, jnp.float32

    prompt = pl.pallas_call(
        functools.partial(gather_kernel, groups, shards),
        out_shape=jax.ShapeDtypeStruct((2, pn, kw), bf16),
        in_specs=[smem, vmem, vmem],
        out_specs=vmem,
        scratch_shapes=[
            VMEM((2, n, kw), bf16), VMEM((groups, 2, n, kw), bf16), VMEM((shards, 2, n, kw), bf16),
            dma((groups,)), dma((groups,)), dma((shards,)), dma((shards,)),
        ],
        compiler_params=pltpu.CompilerParams(collective_id=0, has_side_effects=True),
        name="gather_prompt",
    )(owner, prompt_keys, prompt_values)

    wide = pl.BlockSpec((1, block, group * HEAD_DIM), lambda e: (0, 0, e))
    narrow = pl.BlockSpec((1, block, HEAD_DIM), lambda e: (0, 0, e))
    pair = pl.BlockSpec((2, pn, HEAD_DIM), lambda e: (0, 0, e))
    out, dq, dk, dv, term = pl.pallas_call(
        functools.partial(attend_kernel, group),
        grid=(heads,),
        out_shape=(
            jax.ShapeDtypeStruct(queries.shape, bf16),
            jax.ShapeDtypeStruct(queries.shape, bf16),
            jax.ShapeDtypeStruct(resp_keys.shape, bf16),
            jax.ShapeDtypeStruct(resp_keys.shape, bf16),
            jax.ShapeDtypeStruct((2, pn, kw), bf16),
        ),
        in_specs=[smem, wide, wide, narrow, narrow, pair],
        out_specs=(wide, wide, narrow, narrow, pair),
        scratch_shapes=[
            VMEM((span, HEAD_DIM), bf16), VMEM((span, HEAD_DIM), bf16),
            VMEM((HEAD_DIM, span), bf16), VMEM((HEAD_DIM, span), bf16),
            VMEM((span, HEAD_DIM), f32), VMEM((span, HEAD_DIM), f32),
        ],
        compiler_params=pltpu.CompilerParams(
            dimension_semantics=("arbitrary",), vmem_limit_bytes=56 * 1024 * 1024
        ),
        name="attend",
    )(lengths[here][None], queries, d_out, resp_keys, resp_values, prompt)

    shape = jax.ShapeDtypeStruct(prompt_keys.shape, f32)
    dpk, dpv = pl.pallas_call(
        functools.partial(reduce_kernel, groups, shards),
        out_shape=(shape, shape),
        in_specs=[smem, vmem],
        out_specs=(vmem, vmem),
        scratch_shapes=[
            VMEM((shards, 2, n, kw), bf16), VMEM((2, n, kw), f32),
            VMEM((groups, 2, n, kw), bf16), VMEM((groups, 2, n, kw), bf16),
            dma((shards,)), dma((shards,)), dma((groups,)), dma((groups,)),
        ],
        compiler_params=pltpu.CompilerParams(collective_id=1, has_side_effects=True),
        name="reduce_prompt",
    )(owner, term)
    return out, dq, dk, dv, dpk, dpv


def solution(mesh):
    rows = P(("dp", "rollout"), None, None)
    prompt = P("dp", "rollout", None)
    return jax.shard_map(
        per_device,
        mesh=mesh,
        in_specs=(rows, rows, rows, prompt, prompt, rows, P(), P()),
        out_specs=(rows, rows, rows, rows, prompt, prompt),
        check_vma=False,
    )
```

profile of v0, /device:TPU:0, one launch (start us, length us, event | category | flops | bytes accessed | tf_op | source)
XLA Modules:
  0.0 66.2 jit_solution(15121004336789075223)
XLA Ops:
  0.6 1.2 %dynamic_slice.3.length = s32[1]{0:T(128)} dynamic-slice(s32[32]{0:T(128)} %param.14, s32[]{:T(128)S(6)} %select_n.3), dynamic_slice_sizes={1} | dynamic-slice | bytes 12 | tf_op jit(solution)/shard_map/dynamic_slice | solution.py:227
  1.9 16.4 %gather_prompt.1.prompt = bf16[2,128,512]{2,1,0:T(8,128)(2,1)} custom-call(s32[32]{0:T(128)} %owner.3, bf16[1,16,512]{2,1,0:T(8,128)(2,1)} %pk.1, bf16[1,16,512]{2,1,0:T(8,128)(2,1)} %pv.1), custom_call_target="tpu_custom_call" | custom-call | tf_op jit(solution)/shard_map/gather_prompt/pallas_call | solution.py:190
  18.3 30.7 %attend.1 = (bf16[1,512,2560]{2,1,0:T(8,128)(2,1)}, bf16[1,512,2560]{2,1,0:T(8,128)(2,1)}, bf16[1,512,512]{2,1,0:T(8,128)(2,1)}, bf16[1,512,512]{2,1,0:T(8,128)(2,1)}, bf16[2,128,512]{2,1,0:T(8,128)(2,1)}) custom-call(s32[1]{0:T(128)} %dynamic_slice.3.length, bf16[1,512,2560]{2,1,0:T(8,128)(2,1)} %q.1, bf16[1,512,2560]{2,1,0:T(8,128)(2,1)} %d.1, ...), custom_call_target="tpu_custom_call" | custom-call | tf_op jit(solution)/shard_map/attend/pallas_call | solution.py:206
  49.0 14.5 %reduce_prompt.1 = (f32[1,16,512]{2,1,0:T(8,128)}, f32[1,16,512]{2,1,0:T(8,128)}) custom-call(s32[32]{0:T(128)} %owner.3, bf16[2,128,512]{2,1,0:T(8,128)(2,1)} %get-tuple-element.17.term), custom_call_target="tpu_custom_call" | custom-call | tf_op jit(solution)/shard_map/reduce_prompt/pallas_call | solution.py:230
  63.5 1.4 %copy.16 = f32[1,16,512]{2,1,0:T(8,128)} copy(f32[1,16,512]{2,1,0:T(8,128)} %get-tuple-element.30) | data formatting | bytes 65536
  64.8 1.4 %copy.17 = f32[1,16,512]{2,1,0:T(8,128)} copy(f32[1,16,512]{2,1,0:T(8,128)} %get-tuple-element.31) | data formatting | bytes 65536
where the time goes:
time: 66.6 us; the launch traced here: 66.2 us
  Pallas kernels  61.6 us (92%)
  local copies, waits for them, and re-layouts  3.99 us (6%)
    pallas_call x1, Pallas kernels, per_device(): pl.pallas_call(functools.partial(attend_kernel, group), grid=(heads,), ou...  30.7 us
    pallas_call x1, Pallas kernels, per_device(): pl.pallas_call(functools.partial(gather_kernel, groups, shards), out_shap...  16.4 us
    pallas_call x1, Pallas kernels, per_device(): pl.pallas_call(functools.partial(reduce_kernel, groups, shards), out_shap...  14.5 us
    unnamed x2, local copies, waits for them, and re-layouts  2.75 us

commit v1 on v0

v1 whole, which is shorter than its diff:
```python
import functools
import math

import jax
import jax.numpy as jnp
from jax import lax
from jax.experimental import pallas as pl
from jax.experimental.pallas import tpu as pltpu
from jax.sharding import PartitionSpec as P

HEAD_DIM = 128
MESH = pl.DeviceIdType.MESH
ROWS = 256
VMEM = pltpu.VMEM


def remote(src, dst, send, recv, axis, peer):
    return pltpu.make_async_remote_copy(
        src_ref=src, dst_ref=dst, send_sem=send, recv_sem=recv,
        device_id={axis: peer}, device_id_type=MESH,
    )


def dot(a, b, dims=((1,), (0,))):
    return lax.dot_general(a, b, (dims, ((), ())), preferred_element_type=jnp.float32)


def lanes(e, width):
    return pl.ds(pl.multiple_of(e * width, width), width)


def step_kernel(groups, shards, heads, group,
                owner, lengths, q, d, rk, rv, pk, pv,
                out, dq, dk, dv, dpk, dpv, *scratch):
    held = scratch[:heads]
    (kv, kt, vt, qs, gs, stage, term, got, acc, stage2, got2, dks, dvs,
     lp, lq, s1, r1, s2, r2, s3, r3, s4, r4) = scratch[heads:]
    dp, ro = lax.axis_index("dp"), lax.axis_index("rollout")
    block = q.shape[1]
    span = kv.shape[2]
    pn = span - block
    n = pn // shards
    width = group * HEAD_DIM
    scale = HEAD_DIM ** -0.5
    live_n = lengths[dp * shards + ro]
    row = pl.ds(pl.multiple_of(ro * n, n), n)

    def rows_for(peer):
        return pl.ds(pl.multiple_of(peer * n, n), n)

    barrier = pltpu.get_barrier_semaphore()
    for k in range(1, groups):
        pl.semaphore_signal(
            barrier, inc=1, device_id={"dp": lax.rem(dp + k, groups)}, device_id_type=MESH
        )
    for k in range(1, shards):
        pl.semaphore_signal(
            barrier, inc=1, device_id={"rollout": lax.rem(ro + k, shards)}, device_id_type=MESH
        )

    def prompt_loads(e):
        cols = pl.ds(e * HEAD_DIM, HEAD_DIM)
        return [
            pltpu.make_async_copy(pk.at[0, :, cols], held[e].at[0, 0], lp.at[e, 0]),
            pltpu.make_async_copy(pv.at[0, :, cols], held[e].at[0, 1], lp.at[e, 1]),
        ]

    def loads(e):
        cols = lanes(e, HEAD_DIM)
        wide = lanes(e, width)
        return [
            pltpu.make_async_copy(rk.at[0, :, cols], kv.at[e, 0, pl.ds(pn, block), :], lq.at[e, 0]),
            pltpu.make_async_copy(q.at[0, :, wide], qs.at[e], lq.at[e, 1]),
            pltpu.make_async_copy(rv.at[0, :, cols], kv.at[e, 1, pl.ds(pn, block), :], lq.at[e, 2]),
            pltpu.make_async_copy(d.at[0, :, wide], gs.at[e], lq.at[e, 3]),
        ]

    for e in range(heads):
        for copy in prompt_loads(e):
            copy.start()
    for e in range(heads):
        for copy in loads(e):
            copy.start()
    for e in range(heads):
        for copy in prompt_loads(e):
            copy.wait()
    pl.semaphore_wait(barrier, groups + shards - 2)

    def gather1(e, k):
        return remote(held[e].at[0], held[e].at[k], s1.at[e, k], r1.at[e, k],
                      "dp", lax.rem(dp + k, groups))

    def gather2(e, k):
        return remote(stage.at[e, k], kv.at[e, :, row, :], s2.at[e, k], r2.at[e, k],
                      "rollout", lax.rem(ro + k, shards))

    def reduce1(e, k):
        peer = lax.rem(ro + k, shards)
        return remote(term.at[e, :, rows_for(peer), :], got.at[e, k], s3.at[e, k], r3.at[e, k],
                      "rollout", peer)

    def reduce2(e, k):
        return remote(stage2.at[e, k], got2.at[e, k], s4.at[e, k], r4.at[e, k],
                      "dp", lax.rem(dp + k, groups))

    for e in range(heads):
        for k in range(1, groups):
            gather1(e, k).start()
    for e in range(heads):
        for k in range(1, groups):
            gather1(e, k).wait_recv()

        def rows_of(peer):
            return held[e][lax.rem(dp - owner[dp * shards + peer] + groups, groups)]

        for k in range(1, shards):
            stage[e, k] = rows_of(lax.rem(ro + k, shards))
            gather2(e, k).start()
        kv[e, :, row, :] = rows_of(ro)

    lead = lax.broadcasted_iota(jnp.int32, (ROWS, ROWS), 0) <= lax.broadcasted_iota(
        jnp.int32, (ROWS, ROWS), 1
    )
    c = scale * math.log2(math.e)

    def compute(e):
        kc, vc = kv.at[e, 0], kv.at[e, 1]
        kt[...] = kc[...].T
        vt[...] = vc[...].T
        dks[...] = jnp.zeros_like(dks)
        dvs[...] = jnp.zeros_like(dvs)

        def head(h):
            cols = pl.ds(h * HEAD_DIM, HEAD_DIM)
            at = pl.ds(pl.multiple_of(e * width + h * HEAD_DIM, HEAD_DIM), HEAD_DIM)
            for t in range(block // ROWS):
                rows = pl.ds(t * ROWS, ROWS)
                old, end = pn + t * ROWS, pn + (t + 1) * ROWS
                live = (
                    lax.broadcasted_iota(jnp.int32, (ROWS, HEAD_DIM), 0) + t * ROWS < live_n
                )
                qt = qs[e, rows, cols]
                g = jnp.where(live, gs[e, rows, cols].astype(jnp.float32), 0.0).astype(jnp.bfloat16)
                sa = dot(kc[:old], qt, ((1,), (1,))) * c
                sb = jnp.where(lead, dot(kc[old:end], qt, ((1,), (1,))) * c, -1e30)
                top = jnp.maximum(
                    jnp.max(sa, axis=0, keepdims=True), jnp.max(sb, axis=0, keepdims=True)
                )
                ea, eb = jnp.exp2(sa - top), jnp.exp2(sb - top)
                inv = 1.0 / (
                    jnp.sum(ea, axis=0, keepdims=True) + jnp.sum(eb, axis=0, keepdims=True)
                )
                p = jnp.concatenate([ea, eb], axis=0) * inv
                w = p.astype(jnp.bfloat16)
                o = dot(vt[:, :end], w)
                out[0, rows, at] = jnp.where(live, o.T, 0.0).astype(jnp.bfloat16)
                dpr = dot(vc[:end], g, ((1,), (1,)))
                delta = jnp.sum(p * dpr, axis=0, keepdims=True)
                ds = (p * (dpr - delta)).astype(jnp.bfloat16)
                dq[0, rows, at] = (dot(kt[:, :end], ds) * scale).T.astype(jnp.bfloat16)
                dks[:end] += dot(ds, qt)
                dvs[:end] += dot(w, g)

        for h in range(group):
            head(h)
        dkf = dks[...] * scale
        narrow = lanes(e, HEAD_DIM)
        dk[0, :, narrow] = dkf[pn:].astype(jnp.bfloat16)
        dv[0, :, narrow] = dvs[pn:].astype(jnp.bfloat16)
        term[e, 0] = dkf[:pn].astype(jnp.bfloat16)
        term[e, 1] = dvs[:pn].astype(jnp.bfloat16)

    def collect(e):
        for k in range(1, shards):
            reduce1(e, k).wait_recv()
        got[e, 0] = term[e, :, row, :]
        for k in range(groups):
            target = lax.rem(dp + k, groups)
            total = jnp.zeros(acc.shape[1:], jnp.float32)
            for j in range(shards):
                source = lax.rem(ro - j + shards, shards)
                pick = (owner[dp * shards + source] == target).astype(jnp.float32)
                total = total + pick * got[e, j].astype(jnp.float32)
            if k == 0:
                acc[e] = total
            else:
                stage2[e, k] = total.astype(jnp.bfloat16)
                reduce2(e, k).start()

    def turn(e, carry):
        for copy in loads(e):
            copy.wait()
        for k in range(1, shards):
            gather2(e, k).wait_recv()
        compute(e)
        for k in range(1, shards):
            reduce1(e, k).start()

        @pl.when(e > 0)
        def _():
            collect(e - 1)

        return carry

    lax.fori_loop(0, heads, turn, 0)
    collect(heads - 1)
    for e in range(heads):
        cols = pl.ds(e * HEAD_DIM, HEAD_DIM)
        for k in range(1, groups):
            reduce2(e, k).wait_recv()
        total = acc[e]
        for k in range(1, groups):
            total = total + got2[e, k].astype(jnp.float32)
        dpk[0, :, cols] = total[0]
        dpv[0, :, cols] = total[1]
    for e in range(heads):
        for k in range(1, groups):
            gather1(e, k).wait_send()
            reduce2(e, k).wait_send()
        for k in range(1, shards):
            gather2(e, k).wait_send()
            reduce1(e, k).wait_send()


def flush_kernel(count, *refs):
    sems = refs[-1]
    copies = [pltpu.make_async_copy(refs[i], refs[count + i], sems.at[i]) for i in range(count)]
    for copy in copies:
        copy.start()
    for copy in copies:
        copy.wait()


def per_device(queries, resp_keys, resp_values, prompt_keys, prompt_values, d_out, lengths, owner):
    shards = lax.axis_size("rollout")
    groups = lax.axis_size("dp")
    n, kw = prompt_keys.shape[1:]
    pn = n * shards
    block, qw = queries.shape[1:]
    heads = kw // HEAD_DIM
    group = qw // kw
    span = pn + block
    smem = pl.BlockSpec(memory_space=pltpu.SMEM)
    vmem = pl.BlockSpec(memory_space=pltpu.VMEM)
    anyw = pl.BlockSpec(memory_space=pltpu.HBM)
    dma = pltpu.SemaphoreType.DMA
    bf16, f32 = jnp.bfloat16, jnp.float32
    shapes = [(queries.shape, bf16), (queries.shape, bf16), (resp_keys.shape, bf16),
              (resp_keys.shape, bf16), (prompt_keys.shape, f32), (prompt_keys.shape, f32)]
    results = pl.pallas_call(
        functools.partial(step_kernel, groups, shards, heads, group),
        out_shape=tuple(VMEM(s, t) for s, t in shapes),
        in_specs=[smem, smem] + [anyw] * 6,
        out_specs=(vmem,) * 6,
        scratch_shapes=[VMEM((groups, 2, n, HEAD_DIM), bf16)] * heads + [
            VMEM((heads, 2, span, HEAD_DIM), bf16),
            VMEM((HEAD_DIM, span), bf16), VMEM((HEAD_DIM, span), bf16),
            VMEM((heads, block, group * HEAD_DIM), bf16),
            VMEM((heads, block, group * HEAD_DIM), bf16),
            VMEM((heads, shards, 2, n, HEAD_DIM), bf16),
            VMEM((heads, 2, pn, HEAD_DIM), bf16),
            VMEM((heads, shards, 2, n, HEAD_DIM), bf16),
            VMEM((heads, 2, n, HEAD_DIM), f32),
            VMEM((heads, groups, 2, n, HEAD_DIM), bf16),
            VMEM((heads, groups, 2, n, HEAD_DIM), bf16),
            VMEM((span, HEAD_DIM), f32), VMEM((span, HEAD_DIM), f32),
            dma((heads, 2)), dma((heads, 4)),
            dma((heads, groups)), dma((heads, groups)), dma((heads, shards)), dma((heads, shards)),
            dma((heads, shards)), dma((heads, shards)), dma((heads, groups)), dma((heads, groups)),
        ],
        compiler_params=pltpu.CompilerParams(
            collective_id=0, has_side_effects=True, vmem_limit_bytes=48 * 1024 * 1024
        ),
        name="attend",
    )(owner, lengths, *(pltpu.with_memory_space_constraint(x, pltpu.HBM) for x in (
        queries, d_out, resp_keys, resp_values, prompt_keys, prompt_values)))
    return pl.pallas_call(
        functools.partial(flush_kernel, len(shapes)),
        out_shape=tuple(jax.ShapeDtypeStruct(s, t) for s, t in shapes),
        in_specs=[vmem] * len(shapes),
        out_specs=(anyw,) * len(shapes),
        scratch_shapes=[dma((len(shapes),))],
        compiler_params=pltpu.CompilerParams(vmem_limit_bytes=1024 * 1024),
        name="flush",
    )(*results)


def solution(mesh):
    rows = P(("dp", "rollout"), None, None)
    prompt = P("dp", "rollout", None)
    return jax.shard_map(
        per_device,
        mesh=mesh,
        in_specs=(rows, rows, rows, prompt, prompt, rows, P(), P()),
        out_specs=(rows, rows, rows, rows, prompt, prompt),
        check_vma=False,
    )
```

time: 66.6 us -> 54.4 us (0.82)
  Pallas kernels: 61.6 us -> 53.6 us
  local copies, waits for them, and re-layouts: 3.99 us -> 0 us
    pallas_call x3 -> x2, Pallas kernels: 61.6 us -> 53.6 us  [the longest x1 50.8 us: per_device(): pl.pallas_call(functools.partial(step_kernel, groups, shards, heads, grou...]
    unnamed x2 -> x0, local copies, waits for them, and re-layouts: 2.75 us -> none
    dynamic_slice x1 -> x0, local copies, waits for them, and re-layouts: 1.24 us -> none  [per_device(): lengths[here][None]]
where the time goes in v1:
time: 54.4 us; the launch traced here: 54.2 us
  Pallas kernels  53.6 us (99%)
  between operations  0.64 us (1%)
    pallas_call x1, Pallas kernels, per_device(): pl.pallas_call(functools.partial(step_kernel, groups, shards, heads, grou...  50.8 us
    pallas_call x1, Pallas kernels, per_device(): pl.pallas_call(functools.partial(flush_kernel, len(shapes)), out_shape=tu...  2.74 us

profile of v1, /device:TPU:0, one launch (start us, length us, event | category | flops | bytes accessed | tf_op | source)
XLA Modules:
  0.0 54.2 jit_solution(7465931168477755779)
XLA Ops:
  0.6 50.8 %attend.1 = (bf16[1,512,2560]{2,1,0:T(8,128)(2,1)S(1)}, bf16[1,512,2560]{2,1,0:T(8,128)(2,1)S(1)}, bf16[1,512,512]{2,1,0:T(8,128)(2,1)S(1)}, bf16[1,512,512]{2,1...) custom-call(s32[32]{0:T(128)} %owner.1, s32[32]{0:T(128)} %lengths.1, ...), custom_call_target="tpu_custom_call" | custom-call | tf_op jit(solution)/shard_map/attend/pallas_call | solution.py:250
  51.5 2.7 %flush.1 = (bf16[1,512,2560]{2,1,0:T(8,128)(2,1)}, bf16[1,512,2560]{2,1,0:T(8,128)(2,1)}, bf16[1,512,512]{2,1,0:T(8,128)(2,1)}, bf16[1,512,512]{2,1,0:T(8,128)(2...) custom-call(bf16[1,512,2560]{2,1,0:T(8,128)(2,1)S(1)} %get-tuple-element.12.refs_0_, ...), custom_call_target="tpu_custom_call" | custom-call | tf_op jit(solution)/shard_map/flush/pallas_call | solution.py:277

commit v2 on v1

--- a/solution.py
+++ b/solution.py
@@ -33,8 +33,11 @@
                 owner, lengths, q, d, rk, rv, pk, pv,
                 out, dq, dk, dv, dpk, dpv, *scratch):
     held = scratch[:heads]
+    turns = q.shape[1] // ROWS
+    dss, ws, sr, dr = (scratch[heads + i * turns:heads + (i + 1) * turns] for i in range(4))
     (kv, kt, vt, qs, gs, stage, term, got, acc, stage2, got2, dks, dvs,
-     lp, lq, s1, r1, s2, r2, s3, r3, s4, r4) = scratch[heads:]
+     gsc, qsc, sp, wp, tops, sums, ex,
+     lp, lq, s1, r1, s2, r2, s3, r3, s4, r4) = scratch[heads + 4 * turns:]
     dp, ro = lax.axis_index("dp"), lax.axis_index("rollout")
     block = q.shape[1]
     span = kv.shape[2]
@@ -65,26 +68,25 @@
             pltpu.make_async_copy(pv.at[0, :, cols], held[e].at[0, 1], lp.at[e, 1]),
         ]
 
-    def loads(e):
-        cols = lanes(e, HEAD_DIM)
-        wide = lanes(e, width)
+    def loads(e, i):
+        own, wide = (rk, q) if i == 0 else (rv, d)
+        whole = qs if i == 0 else gs
         return [
-            pltpu.make_async_copy(rk.at[0, :, cols], kv.at[e, 0, pl.ds(pn, block), :], lq.at[e, 0]),
-            pltpu.make_async_copy(q.at[0, :, wide], qs.at[e], lq.at[e, 1]),
-            pltpu.make_async_copy(rv.at[0, :, cols], kv.at[e, 1, pl.ds(pn, block), :], lq.at[e, 2]),
-            pltpu.make_async_copy(d.at[0, :, wide], gs.at[e], lq.at[e, 3]),
+            pltpu.make_async_copy(
+                own.at[0, :, lanes(e, HEAD_DIM)], kv.at[e, i, pl.ds(pn, block), :], lq.at[e, 2 * i]
+            ),
+            pltpu.make_async_copy(
+                wide.at[0, :, lanes(e, width)], whole.at[e], lq.at[e, 2 * i + 1]
+            ),
         ]
 
     for e in range(heads):
         for copy in prompt_loads(e):
             copy.start()
     for e in range(heads):
-        for copy in loads(e):
-            copy.start()
-    for e in range(heads):
-        for copy in prompt_loads(e):
-            copy.wait()
-    pl.semaphore_wait(barrier, groups + shards - 2)
+        for i in range(2):
+            for copy in loads(e, i):
+                copy.start()
 
     def gather1(e, k):
         return remote(held[e].at[0], held[e].at[k], s1.at[e, k], r1.at[e, k],
@@ -103,72 +105,166 @@
         return remote(stage2.at[e, k], got2.at[e, k], s4.at[e, k], r4.at[e, k],
                       "dp", lax.rem(dp + k, groups))
 
-    for e in range(heads):
-        for k in range(1, groups):
-            gather1(e, k).start()
-    for e in range(heads):
-        for k in range(1, groups):
-            gather1(e, k).wait_recv()
-
-        def rows_of(peer):
-            return held[e][lax.rem(dp - owner[dp * shards + peer] + groups, groups)]
-
-        for k in range(1, shards):
-            stage[e, k] = rows_of(lax.rem(ro + k, shards))
-            gather2(e, k).start()
-        kv[e, :, row, :] = rows_of(ro)
-
     lead = lax.broadcasted_iota(jnp.int32, (ROWS, ROWS), 0) <= lax.broadcasted_iota(
         jnp.int32, (ROWS, ROWS), 1
     )
     c = scale * math.log2(math.e)
 
-    def compute(e):
-        kc, vc = kv.at[e, 0], kv.at[e, 1]
-        kt[...] = kc[...].T
-        vt[...] = vc[...].T
+    items = [(h, t) for h in range(group) for t in range(turns)]
+
+    def response_part(e):
+        for i in range(2):
+            for copy in loads(e, i):
+                copy.wait()
+        peaks = [None] * len(items)
+
+        def scores(i):
+            h, t = items[i]
+            qt = qs[e, pl.ds(t * ROWS, ROWS), pl.ds(h * HEAD_DIM, HEAD_DIM)]
+            old, end = t * ROWS, (t + 1) * ROWS
+            sb = jnp.where(lead, dot(kv[e, 0, pn + old:pn + end], qt, ((1,), (1,))), -1e30)
+            top = jnp.max(sb, axis=0, keepdims=True)
+            sr[t][e * group + h, old:end] = sb
+            if t:
+                sa = dot(kv[e, 0, pn:pn + old], qt, ((1,), (1,)))
+                top = jnp.maximum(top, jnp.max(sa, axis=0, keepdims=True))
+                sr[t][e * group + h, :old] = sa
+            peaks[i] = top * c
+            tops[e, pl.ds(i, 1), :] = peaks[i]
+
+        def powers(i):
+            h, t = items[i]
+            x = jnp.exp2(sr[t][e * group + h] * c - peaks[i])
+            sums[e, pl.ds(i, 1), :] = jnp.sum(x, axis=0, keepdims=True)
+            sr[t][e * group + h] = x
+            ws[t][e * group + h] = x.astype(jnp.bfloat16)
+
+        def prob_grads(i):
+            h, t = items[i]
+            rows = pl.ds(t * ROWS, ROWS)
+            live = lax.broadcasted_iota(jnp.int32, (ROWS, HEAD_DIM), 0) + t * ROWS < live_n
+            g = jnp.where(live, gs[e, rows, pl.ds(h * HEAD_DIM, HEAD_DIM)].astype(jnp.float32), 0.0)
+            dr[t][e * group + h] = dot(
+                kv[e, 1, pn:pn + (t + 1) * ROWS], g.astype(jnp.bfloat16), ((1,), (1,))
+            )
+
+        for s in range(len(items) + 1):
+            if s < len(items):
+                scores(s)
+                if e < heads - 1:
+                    prob_grads(s)
+            if s:
+                powers(s - 1)
+
+    def attend(e, last):
+        info = [{} for _ in items]
+        kt[...] = kv[e, 0].T
+        vt[...] = kv[e, 1].T
+
+        def place(i):
+            h, t = items[i]
+            cols = pl.ds(h * HEAD_DIM, HEAD_DIM)
+            at = pl.ds(pl.multiple_of(e * width + h * HEAD_DIM, HEAD_DIM), HEAD_DIM)
+            return h, t, cols, at, pl.ds(t * ROWS, ROWS), (t + 1) * ROWS
+
+        def prompt_scores(i):
+            h, t, cols, at, rows, end = place(i)
+            s = dot(kv[e, 0, :pn], qs[e, rows, cols], ((1,), (1,)))
+            sp[i % 2] = s
+            own = tops[e, pl.ds(i, 1), :]
+            top = jnp.maximum(jnp.max(s, axis=0, keepdims=True) * c, own)
+            info[i]["top"] = top
+            info[i]["part"] = jnp.exp2(own - top)
+
+        def weigh(i):
+            h, t, cols, at, rows, end = place(i)
+            x = jnp.exp2(sp[i % 2] * c - info[i]["top"])
+            total = jnp.sum(x, axis=0, keepdims=True) + sums[e, pl.ds(i, 1), :] * info[i]["part"]
+            info[i]["inv"] = 1.0 / total
+            ex[i % 3] = x
+            wp[i % 4] = x.astype(jnp.bfloat16)
+
+        def forward(i):
+            h, t, cols, at, rows, end = place(i)
+            inv, part = info[i]["inv"], info[i]["part"]
+            o = dot(vt[:, :pn], wp[i % 4]) * inv
+            o = o + dot(vt[:, pn:pn + end], ws[t][e * group + h]) * (inv * part)
+            live = lax.broadcasted_iota(jnp.int32, (HEAD_DIM, ROWS), 1) + t * ROWS < live_n
+            gt = jnp.where(live, gs[e, rows, cols].T.astype(jnp.float32), 0.0)
+            info[i]["delta"] = jnp.sum(o * gt, axis=0, keepdims=True)
+            info[i]["gt"] = gt.astype(jnp.bfloat16)
+            out[0, rows, at] = jnp.where(live, o, 0.0).astype(jnp.bfloat16).T
+            gi = gt * inv
+            qi = qs[e, rows, cols].T.astype(jnp.float32) * (inv * scale)
+            gsc[0, h, t] = gi.astype(jnp.bfloat16).T
+            qsc[0, h, t] = qi.astype(jnp.bfloat16).T
+            gsc[1, h, t] = (gi * part).astype(jnp.bfloat16).T
+            qsc[1, h, t] = (qi * part).astype(jnp.bfloat16).T
+
+        def score_grads(i):
+            h, t, cols, at, rows, end = place(i)
+            delta = info[i]["delta"]
+            dpr = dot(kv[e, 1, :pn], info[i]["gt"])
+            dss[t][h, :pn] = (ex[i % 3] * (dpr - delta)).astype(jnp.bfloat16)
+            if last:
+                dpr = dot(kv[e, 1, pn:pn + end], info[i]["gt"])
+            else:
+                dpr = dr[t][e * group + h]
+            x = sr[t][e * group + h] * (dpr - delta)
+            dss[t][h, pn:] = x.astype(jnp.bfloat16)
+
+        def query_grads(i):
+            h, t, cols, at, rows, end = place(i)
+            factor = info[i]["inv"] * scale
+            grad = dot(kt[:, :pn], dss[t][h, :pn]) * factor
+            grad = grad + dot(kt[:, pn:pn + end], dss[t][h, pn:]) * (factor * info[i]["part"])
+            dq[0, rows, at] = grad.astype(jnp.bfloat16).T
+
+        def backward(i):
+            h, t, cols, at, rows, end = place(i)
+            dks[:pn] += dot(dss[t][h, :pn], qsc[0, h, t])
+            dvs[:pn] += dot(wp[i % 4], gsc[0, h, t])
+            if not last:
+                dks[pn:pn + end] += dot(dss[t][h, pn:], qsc[1, h, t])
+                dvs[pn:pn + end] += dot(ws[t][e * group + h], gsc[1, h, t])
+                query_grads(i)
+
         dks[...] = jnp.zeros_like(dks)
         dvs[...] = jnp.zeros_like(dvs)
-
-        def head(h):
-            cols = pl.ds(h * HEAD_DIM, HEAD_DIM)
-            at = pl.ds(pl.multiple_of(e * width + h * HEAD_DIM, HEAD_DIM), HEAD_DIM)
-            for t in range(block // ROWS):
-                rows = pl.ds(t * ROWS, ROWS)
-                old, end = pn + t * ROWS, pn + (t + 1) * ROWS
-                live = (
-                    lax.broadcasted_iota(jnp.int32, (ROWS, HEAD_DIM), 0) + t * ROWS < live_n
-                )
-                qt = qs[e, rows, cols]
-                g = jnp.where(live, gs[e, rows, cols].astype(jnp.float32), 0.0).astype(jnp.bfloat16)
-                sa = dot(kc[:old], qt, ((1,), (1,))) * c
-                sb = jnp.where(lead, dot(kc[old:end], qt, ((1,), (1,))) * c, -1e30)
-                top = jnp.maximum(
-                    jnp.max(sa, axis=0, keepdims=True), jnp.max(sb, axis=0, keepdims=True)
-                )
-                ea, eb = jnp.exp2(sa - top), jnp.exp2(sb - top)
-                inv = 1.0 / (
-                    jnp.sum(ea, axis=0, keepdims=True) + jnp.sum(eb, axis=0, keepdims=True)
-                )
-                p = jnp.concatenate([ea, eb], axis=0) * inv
-                w = p.astype(jnp.bfloat16)
-                o = dot(vt[:, :end], w)
-                out[0, rows, at] = jnp.where(live, o.T, 0.0).astype(jnp.bfloat16)
-                dpr = dot(vc[:end], g, ((1,), (1,)))
-                delta = jnp.sum(p * dpr, axis=0, keepdims=True)
-                ds = (p * (dpr - delta)).astype(jnp.bfloat16)
-                dq[0, rows, at] = (dot(kt[:, :end], ds) * scale).T.astype(jnp.bfloat16)
-                dks[:end] += dot(ds, qt)
-                dvs[:end] += dot(w, g)
-
-        for h in range(group):
-            head(h)
-        dkf = dks[...] * scale
+        stages = ((prompt_scores, 0), (score_grads, 3), (backward, 4), (forward, 2), (weigh, 1))
+        for s in range(len(items) + 4):
+            for stage_fn, late in stages:
+                if 0 <= s - late < len(items):
+                    stage_fn(s - late)
+        term[e, 0] = dks[:pn].astype(jnp.bfloat16)
+        term[e, 1] = dvs[:pn].astype(jnp.bfloat16)
+        for k in range(1, shards):
+            reduce1(e, k).start()
         narrow = lanes(e, HEAD_DIM)
-        dk[0, :, narrow] = dkf[pn:].astype(jnp.bfloat16)
-        dv[0, :, narrow] = dvs[pn:].astype(jnp.bfloat16)
-        term[e, 0] = dkf[:pn].astype(jnp.bfloat16)
-        term[e, 1] = dvs[:pn].astype(jnp.bfloat16)
+        if not last:
+            dk[0, :, narrow] = dks[pn:].astype(jnp.bfloat16)
+            dv[0, :, narrow] = dvs[pn:].astype(jnp.bfloat16)
+            return None
+
+        def key_grads(t0):
+            sk = sv = 0.0
+            for h, t in items:
+                if t >= t0:
+                    sk = sk + dot(dss[t][h, pl.ds(pn + t0 * ROWS, ROWS)], qsc[1, h, t])
+                    sv = sv + dot(ws[t][e * group + h, pl.ds(t0 * ROWS, ROWS)], gsc[1, h, t])
+            dk[0, pl.ds(t0 * ROWS, ROWS), narrow] = sk.astype(jnp.bfloat16)
+            dv[0, pl.ds(t0 * ROWS, ROWS), narrow] = sv.astype(jnp.bfloat16)
+
+        def rest_a():
+            for i in range(len(items)):
+                query_grads(i)
+            key_grads(0)
+
+        def rest_b():
+            for t0 in range(1, turns):
+                key_grads(t0)
+
+        return rest_a, rest_b
 
     def collect(e):
         for k in range(1, shards):
@@ -187,14 +283,25 @@
                 stage2[e, k] = total.astype(jnp.bfloat16)
                 reduce2(e, k).start()
 
-    def turn(e, carry):
-        for copy in loads(e):
-            copy.wait()
+    def exchange(e):
+        for k in range(1, groups):
+            gather1(e, k).wait_recv()
+
+        def rows_of(peer):
+            return held[e][lax.rem(dp - owner[dp * shards + peer] + groups, groups)]
+
+        for k in range(1, shards):
+            stage[e, k] = rows_of(lax.rem(ro + k, shards))
+            gather2(e, k).start()
+        kv[e, :, row, :] = rows_of(ro)
+
+    def ready(e):
         for k in range(1, shards):
             gather2(e, k).wait_recv()
-        compute(e)
-        for k in range(1, shards):
-            reduce1(e, k).start()
+
+    def turn(e, carry):
+        ready(e)
+        attend(e, False)
 
         @pl.when(e > 0)
         def _():
@@ -202,8 +309,29 @@
 
         return carry
 
-    lax.fori_loop(0, heads, turn, 0)
-    collect(heads - 1)
+    response_part(0)
+    for e in range(heads):
+        for copy in prompt_loads(e):
+            copy.wait()
+    pl.semaphore_wait(barrier, groups + shards - 2)
+    for e in range(heads):
+        for k in range(1, groups):
+            gather1(e, k).start()
+    cut = heads // 2
+    for e in range(1, cut):
+        response_part(e)
+    for e in range(heads):
+        exchange(e)
+    for e in range(cut, heads):
+        response_part(e)
+    final = heads - 1
+    lax.fori_loop(0, final, turn, 0)
+    ready(final)
+    rest_a, rest_b = attend(final, True)
+    collect(final - 1)
+    rest_a()
+    collect(final)
+    rest_b()
     for e in range(heads):
         cols = pl.ds(e * HEAD_DIM, HEAD_DIM)
         for k in range(1, groups):
@@ -240,6 +368,7 @@
     heads = kw // HEAD_DIM
     group = qw // kw
     span = pn + block
+    ends = range(ROWS, block + 1, ROWS)
     smem = pl.BlockSpec(memory_space=pltpu.SMEM)
     vmem = pl.BlockSpec(memory_space=pltpu.VMEM)
     anyw = pl.BlockSpec(memory_space=pltpu.HBM)
@@ -253,6 +382,11 @@
         in_specs=[smem, smem] + [anyw] * 6,
         out_specs=(vmem,) * 6,
         scratch_shapes=[VMEM((groups, 2, n, HEAD_DIM), bf16)] * heads + [
+            VMEM((group, pn + t, ROWS), bf16) for t in ends
+        ] + [
+            VMEM((count * group, t, ROWS), kind)
+            for count, kind in ((heads, bf16), (heads, f32), (heads - 1, f32)) for t in ends
+        ] + [
             VMEM((heads, 2, span, HEAD_DIM), bf16),
             VMEM((HEAD_DIM, span), bf16), VMEM((HEAD_DIM, span), bf16),
             VMEM((heads, block, group * HEAD_DIM), bf16),
@@ -264,12 +398,18 @@
             VMEM((heads, groups, 2, n, HEAD_DIM), bf16),
             VMEM((heads, groups, 2, n, HEAD_DIM), bf16),
             VMEM((span, HEAD_DIM), f32), VMEM((span, HEAD_DIM), f32),
+            VMEM((2, group, len(ends), ROWS, HEAD_DIM), bf16),
+            VMEM((2, group, len(ends), ROWS, HEAD_DIM), bf16),
+            VMEM((2, pn, ROWS), f32), VMEM((4, pn, ROWS), bf16),
+            VMEM((heads, group * len(ends), ROWS), f32),
+            VMEM((heads, group * len(ends), ROWS), f32),
+            VMEM((3, pn, ROWS), f32),
             dma((heads, 2)), dma((heads, 4)),
             dma((heads, groups)), dma((heads, groups)), dma((heads, shards)), dma((heads, shards)),
             dma((heads, shards)), dma((heads, shards)), dma((heads, groups)), dma((heads, groups)),
         ],
         compiler_params=pltpu.CompilerParams(
-            collective_id=0, has_side_effects=True, vmem_limit_bytes=48 * 1024 * 1024
+            collective_id=0, has_side_effects=True, vmem_limit_bytes=60_600_000
         ),
         name="attend",
     )(owner, lengths, *(pltpu.with_memory_space_constraint(x, pltpu.HBM) for x in (

time: 54.4 us -> 41.4 us (0.76)
  Pallas kernels: 53.6 us -> 40.4 us
    pallas_call x1, Pallas kernels: 50.8 us -> 37.7 us  [per_device(): pl.pallas_call(functools.partial(step_kernel, groups, shards, heads, grou...]
where the time goes in v2:
time: 41.4 us; the launch traced here: 41.2 us
  Pallas kernels  40.4 us (98%)
  between operations  0.8 us (2%)
    pallas_call x1, Pallas kernels, per_device(): pl.pallas_call(functools.partial(step_kernel, groups, shards, heads, grou...  37.7 us
    pallas_call x1, Pallas kernels, per_device(): pl.pallas_call(functools.partial(flush_kernel, len(shapes)), out_shape=tu...  2.74 us

profile of v2, /device:TPU:0, one launch (start us, length us, event | category | flops | bytes accessed | tf_op | source)
XLA Modules:
  0.0 41.2 jit_solution(17186270385137638805)
XLA Ops:
  0.6 37.7 %attend.1 = (bf16[1,512,2560]{2,1,0:T(8,128)(2,1)S(1)}, bf16[1,512,2560]{2,1,0:T(8,128)(2,1)S(1)}, bf16[1,512,512]{2,1,0:T(8,128)(2,1)S(1)}, bf16[1,512,512]{2,1...) custom-call(s32[32]{0:T(128)} %owner.1, s32[32]{0:T(128)} %lengths.1, ...), custom_call_target="tpu_custom_call" | custom-call | tf_op jit(solution)/shard_map/attend/pallas_call | solution.py:379
  38.3 2.7 %flush.1 = (bf16[1,512,2560]{2,1,0:T(8,128)(2,1)}, bf16[1,512,2560]{2,1,0:T(8,128)(2,1)}, bf16[1,512,512]{2,1,0:T(8,128)(2,1)}, bf16[1,512,512]{2,1,0:T(8,128)(2...) custom-call(bf16[1,512,2560]{2,1,0:T(8,128)(2,1)S(1)} %get-tuple-element.12.refs_0_, ...), custom_call_target="tpu_custom_call" | custom-call | tf_op jit(solution)/shard_map/flush/pallas_call | solution.py:417
